TPU v7x, 8 devices: a whole 2x2x1 slice. The times are simulated.
8 devices in a mesh: seqs: 2 (over z, y), states: 4 (over x, core).
Axes of the slice: x: 2, y: 2, z: 1, core: 2. Of those that a mesh axis runs over, the one named last changes fastest.
Arguments:
- trans_mat: bfloat16 [8192, 8192], P(None, 'states')
- emit_mat: bfloat16 [8192, 10000], P('states')
- init_prob: float32 [8192], P('states')
- tokens: int32 [64, 64], P('seqs'), parts along dimension 0
- lengths: int32 [64], P('seqs'), parts along dimension 0
Outputs:
- output 1: float32 [64], P('seqs'), parts along dimension 0
- output 2: float32 [64, 8192], P('seqs', 'states'), parts along dimension 0
- output 3: float32 [16384, 2048], P(('seqs', 'states')), parts along dimension 0
There are 2 independent parts. A program takes and returns all parts, laid end to end along the dimension named above; an argument that names none is the same for every part.
All inputs are finite; a program needn't handle non-finite values.
Results may differ from a plain program's by a relative error of at most 0.001.
Values are sent between devices in bfloat16 or wider.
A program may use at most 1 GiB of HBM per device.

v0:
```python
import jax
import jax.numpy as jnp
from jax import lax
from jax.experimental import pallas as pl
from jax.experimental.pallas import tpu as pltpu
from jax.sharding import PartitionSpec as P

MESH = pl.DeviceIdType.MESH
LOADS = 8
TILE = 256
SLOTS = 4
COPIES = 4


def entry_barrier(others):
    barrier = pltpu.get_barrier_semaphore()
    for other in others:
        pl.semaphore_signal(barrier, inc=1, device_id=other, device_id_type=MESH)
    pl.semaphore_wait(barrier, len(others))


def cols(c):
    return pl.ds(c * TILE, TILE)


class Exchange:
    def __init__(self, me, xbuf, mat, acc, send_sem, recv_sem):
        self.me, self.xbuf, self.mat, self.acc = me, xbuf, mat, acc
        self.send_sem, self.recv_sem = send_sem, recv_sem
        self.block = xbuf.shape[3]
        self.partner = me + 1 - 2 * (me % 2)
        self.cross = 3 - me
        self.far = (me + 2) % 4
        quarter = self.block // 4
        self.pieces = [(k * quarter, quarter) for k in range(3)] + [(3 * quarter, quarter // 2), (3 * quarter + quarter // 2, quarter // 2)]

    def copy(self, slot, owner, k, kind, device):
        lo, size = self.pieces[k]
        ref = self.xbuf.at[slot, owner, :, pl.ds(lo, size)]
        return pltpu.make_async_remote_copy(
            src_ref=ref, dst_ref=ref, send_sem=self.send_sem.at[slot, kind, k], recv_sem=self.recv_sem.at[slot, kind, k],
            device_id={"states": device}, device_id_type=MESH)

    def send(self, slot, k, more):
        @pl.when(more)
        def _():
            self.copy(slot, self.me, k, 1, self.cross).start()
            self.copy(slot, self.me, k, 0, self.partner).start()

    def wait_sends(self, slot):
        for k in range(len(self.pieces)):
            self.copy(slot, self.me, k, 1, self.cross).wait_send()
            self.copy(slot, self.me, k, 0, self.partner).wait_send()
            self.copy(slot, self.cross, k, 2, self.partner).wait_send()

    def product(self, slot, owner, lo, size, first=False, last=False):
        lhs = self.xbuf[slot, owner, :, pl.ds(lo, size)]
        seqs = lhs.shape[0]
        rows = pl.ds(pl.multiple_of(owner * self.block + lo, 128), size)
        if last:
            self.acc[:seqs] += jnp.dot(lhs, self.mat[rows, :], preferred_element_type=jnp.float32)
        else:
            prod = jnp.dot(jnp.concatenate([lhs] * COPIES, axis=0), self.mat[rows, :], preferred_element_type=jnp.float32)
            self.acc[...] = prod if first else self.acc[...] + prod

    def run(self, slot, meanwhile):
        count = len(self.pieces)
        meanwhile()
        self.product(slot, self.me, 0, self.block, first=True)
        for k in range(count):
            self.copy(slot, self.partner, k, 0, self.partner).wait_recv()
        self.product(slot, self.partner, 0, self.block)
        for k in range(count + 1):
            if k < count:
                self.copy(slot, self.cross, k, 1, self.cross).wait_recv()
                self.copy(slot, self.cross, k, 2, self.partner).start()
                self.product(slot, self.cross, *self.pieces[k])
            if k:
                self.copy(slot, self.far, k - 1, 2, self.partner).wait_recv()
                self.product(slot, self.far, *self.pieces[k - 1], last=k == count)


def packed(col):
    group = lax.broadcasted_iota(jnp.int32, (8, 128), 1) // 32
    out = jnp.broadcast_to(col[24:32], (8, 128))
    for k in range(3):
        out = jnp.where(group == k, jnp.broadcast_to(col[8 * k:8 * k + 8], (8, 128)), out)
    return out


def unpacked(tile):
    return jnp.concatenate([tile[:, 32 * k:32 * k + 1] for k in range(4)], axis=0)


def forward_kernel(emit_ref, init_ref, len_col, len_pack, a_hbm, hist_ref, scale_ref, log_ref, post_ref, rows_hbm,
                   mat, xbuf, acc, cbuf, load_sem, send_sem, recv_sem, csend_sem, crecv_sem,
                   over_send, over_recv, turn_send, turn_recv, near_send, near_recv):
    me, seq = lax.axis_index("states"), lax.axis_index("seqs")
    partner, cross, far = me + 1 - 2 * (me % 2), 3 - me, (me + 2) % 4
    steps, seqs, block = emit_ref.shape
    chunks = block // TILE
    rows = mat.shape[0] // LOADS
    loads = [pltpu.make_async_copy(a_hbm.at[pl.ds(k * rows, rows)], mat.at[pl.ds(k * rows, rows)], load_sem.at[k]) for k in range(LOADS)]
    for load in loads:
        load.start()
    entry_barrier([{"states": partner}, {"states": cross}, {"states": far}, {"seqs": 1 - seq}])

    half = block // 2
    piece = half // steps
    others = ((0, cross), (1, far))

    def over(b, kind, owner, other):
        lo = seq * half + b * piece
        return pltpu.make_async_remote_copy(
            src_ref=a_hbm.at[pl.ds(other * block + lo, piece)], dst_ref=rows_hbm.at[owner, pl.ds(lo, piece)],
            send_sem=over_send.at[b % 3, kind], recv_sem=over_recv.at[b % 3, kind], device_id={"states": other}, device_id_type=MESH)

    def turn(b, kind, owner):
        ref = rows_hbm.at[owner, pl.ds(seq * half + b * piece, piece)]
        return pltpu.make_async_remote_copy(
            src_ref=ref, dst_ref=ref, send_sem=turn_send.at[b % 2, kind], recv_sem=turn_recv.at[kind],
            device_id={"seqs": 1 - seq}, device_id_type=MESH)

    def near(b):
        return pltpu.make_async_remote_copy(
            src_ref=a_hbm.at[pl.ds(partner * block + b * 2 * piece, 2 * piece)], dst_ref=rows_hbm.at[me, pl.ds(b * 2 * piece, 2 * piece)],
            send_sem=near_send.at[b % 2], recv_sem=near_recv, device_id={"states": partner}, device_id_type=MESH)

    def rows_start(b):
        for kind, other in others:
            over(b, kind, me, other).start()
        near(b).start()

    def rows_turn(b):
        near(b).wait_send()
        for kind, other in others:
            over(b, kind, me, other).wait_send()
            over(b, kind, other, other).wait_recv()
            turn(b, kind, other).start()

    def rows_end(b):
        for kind, other in others:
            turn(b, kind, other).wait_send()

    def norm_copy(owner, kind, device):
        return pltpu.make_async_remote_copy(
            src_ref=cbuf.at[owner], dst_ref=cbuf.at[owner], send_sem=csend_sem.at[kind], recv_sem=crecv_sem.at[kind],
            device_id={"states": device}, device_id_type=MESH)

    everyone = tuple(enumerate((far, cross, partner)))

    def norm_start(sums):
        cbuf[me] = packed(jnp.sum(sums, axis=1, keepdims=True))
        for kind, other in everyone:
            norm_copy(me, kind, other).start()

    def norm_end():
        for kind, other in everyone:
            norm_copy(other, kind, other).wait_recv()
        for kind, other in everyone:
            norm_copy(me, kind, other).wait_send()
        return cbuf[0] + cbuf[1] + cbuf[2] + cbuf[3]

    def body():
        ex = Exchange(me, xbuf, mat, acc, send_sem, recv_sem)
        ends = {(lo + size) // TILE - 1: k for k, (lo, size) in enumerate(ex.pieces)}

        def finish_step(t, total):
            inv = jnp.broadcast_to(unpacked(1.0 / total), (seqs, TILE))
            live = t < jnp.broadcast_to(len_col[...], (seqs, TILE))
            for n in range(chunks):
                alpha = jnp.where(live, acc[:seqs, cols(n)] * inv, post_ref[:, cols(n)])
                post_ref[:, cols(n)] = alpha
                low = alpha.astype(jnp.bfloat16)
                xbuf[t % SLOTS, me, :, cols(n)] = low
                hist_ref[(t + 1) % steps, :, cols(n)] = low
                if n in ends:
                    ex.send(t % SLOTS, ends[n], t < steps - 1)

        def fold(n, mass, sums):
            acc[:seqs, cols(n)] = mass
            return sums + mass[:, :128] + mass[:, 128:]

        sums = jnp.zeros((seqs, 128), jnp.float32)
        for n in range(chunks):
            sums = fold(n, init_ref[:, cols(n)] * emit_ref[0, :, cols(n)].astype(jnp.float32), sums)
        norm_start(sums)
        rows_start(0)
        post_ref[...] = jnp.zeros_like(post_ref)
        total = norm_end()
        scale_ref[0] = total
        log_ref[...] = jnp.log(total)
        finish_step(0, total)
        for load in loads:
            load.wait()

        def step(t, carry):
            slot = (t - 1) % SLOTS

            ex.run(slot, lambda: rows_start(t))
            sums = jnp.zeros((seqs, 128), jnp.float32)
            for n in range(chunks):
                sums = fold(n, acc[:seqs, cols(n)] * emit_ref[t, :, cols(n)].astype(jnp.float32), sums)
            norm_start(sums)
            rows_turn(t - 1)

            @pl.when(t > 1)
            def _():
                rows_end(t - 2)
                ex.wait_sends((t - 2) % SLOTS)

            total = norm_end()
            finish_step(t, total)
            scale = jnp.where(t < len_pack[...], total, 1.0)
            scale_ref[t] = scale
            log_ref[...] += jnp.log(scale)
            return carry

        lax.fori_loop(1, steps, step, 0)
        ex.wait_sends((steps - 2) % SLOTS)

    body()
    rows_turn(steps - 1)
    rows_end(steps - 2)
    rows_end(steps - 1)

    def landed(ref, sem):
        pltpu.make_async_copy(ref, ref, sem).wait()

    for kind, other in others:
        landed(rows_hbm.at[other, pl.ds((1 - seq) * half, half)], turn_recv.at[kind])
    landed(rows_hbm.at[partner], near_recv)


def forward(emit_seq, init_loc, col, pack, trans_loc):
    steps, seqs, block = emit_seq.shape
    full = trans_loc.shape[0]
    vmem, hbm = pl.BlockSpec(memory_space=pltpu.VMEM), pl.BlockSpec(memory_space=pltpu.HBM)
    dma = pltpu.SemaphoreType.DMA
    return pl.pallas_call(
        forward_kernel,
        out_shape=[
            jax.ShapeDtypeStruct((steps, seqs, block), jnp.bfloat16),
            jax.ShapeDtypeStruct((steps, 8, 128), jnp.float32),
            jax.ShapeDtypeStruct((8, 128), jnp.float32),
            jax.ShapeDtypeStruct((seqs, block), jnp.float32),
            jax.ShapeDtypeStruct((full // block, block, block), jnp.bfloat16),
        ],
        in_specs=[vmem] * 4 + [hbm],
        out_specs=[vmem] * 4 + [hbm],
        scratch_shapes=[
            pltpu.VMEM((full, block), jnp.bfloat16),
            pltpu.VMEM((SLOTS, 4, seqs, block), jnp.bfloat16),
            pltpu.VMEM((COPIES * seqs, block), jnp.float32),
            pltpu.VMEM((4, 8, 128), jnp.float32),
            dma((LOADS,)), dma((SLOTS, 3, 5)), dma((SLOTS, 3, 5)), dma((3,)), dma((3,)),
            dma((3, 2)), dma((3, 2)), dma((2, 2)), dma((2,)), dma((2,)), dma,
        ],
        compiler_params=pltpu.CompilerParams(collective_id=0, has_side_effects=True, vmem_limit_bytes=60 * 1024 * 1024),
        name="forward",
    )(emit_seq, init_loc[None, :], col, pack, trans_loc)


def backward_kernel(emit_ref, scale_ref, len_col, a_hbm, rows_hbm, hist_ref, mat, xbuf, coef, acc, load_sem, send_sem, recv_sem):
    me = lax.axis_index("states")
    partner, cross, far = me + 1 - 2 * (me % 2), 3 - me, (me + 2) % 4
    steps, seqs, block = emit_ref.shape
    chunks = block // TILE
    owners = (me, partner, cross, far)
    loads = []
    for k, owner in enumerate(owners):
        src = a_hbm.at[pl.ds(me * block, block)] if k == 0 else rows_hbm.at[owner]
        loads.append(pltpu.make_async_copy(src, mat.at[pl.ds(owner * block, block)], load_sem.at[k]))
        loads[-1].start()
    entry_barrier([{"states": partner}, {"states": cross}, {"states": far}])

    def weigh(t):
        inv = jnp.where(t < len_col[...], unpacked(1.0 / scale_ref[t]), 0.0)
        coef[...] = emit_ref[t].astype(jnp.float32) * inv

    weigh(steps - 1)
    hist_ref[0] = jnp.zeros(hist_ref.shape[1:], hist_ref.dtype)

    def flips():
        side = block // TILE
        for owner, load in zip(owners, loads):
            load.wait()

            def flip_row(r, carry):
                def flip(c, inner):
                    def tile(p, q):
                        return pl.ds(pl.multiple_of(owner * block + p * TILE, TILE), TILE), pl.ds(pl.multiple_of(q * TILE, TILE), TILE)

                    upper, lower = mat[tile(r, c)], mat[tile(c, r)]
                    mat[tile(r, c)] = lower.T
                    mat[tile(c, r)] = upper.T
                    return inner

                return lax.fori_loop(r, side, flip, carry)

            lax.fori_loop(0, side, flip_row, 0)

    def body():
        ex = Exchange(me, xbuf, mat, acc, send_sem, recv_sem)
        ends = {(lo + size) // TILE - 1: k for k, (lo, size) in enumerate(ex.pieces)}

        def emit_weight(t, n, weight):
            low = weight.astype(jnp.bfloat16)
            xbuf[t % SLOTS, me, :, cols(n)] = low
            hist_ref[t, :, cols(n)] = low
            if n in ends:
                ex.send(t % SLOTS, ends[n], t > 1)

        for n in range(chunks):
            emit_weight(steps - 1, n, coef[:, cols(n)])
        flips()

        def step(k, carry):
            t = steps - 1 - k
            weigh(t - 1)

            ex.run(t % SLOTS, lambda: None)
            dead = jnp.where(t < jnp.broadcast_to(len_col[...], (seqs, TILE)), 0.0, 1.0)
            for n in range(chunks):
                emit_weight(t - 1, n, coef[:, cols(n)] * (acc[:seqs, cols(n)] + dead))

            @pl.when(k > 0)
            def _():
                ex.wait_sends((t + 1) % SLOTS)

            return carry

        lax.fori_loop(0, steps - 2, step, 0)
        ex.wait_sends(2 % SLOTS)

    body()


def backward(emit_seq, scales, col, trans_loc, rows_loc):
    steps, seqs, block = emit_seq.shape
    full = trans_loc.shape[0]
    vmem, hbm = pl.BlockSpec(memory_space=pltpu.VMEM), pl.BlockSpec(memory_space=pltpu.HBM)
    dma = pltpu.SemaphoreType.DMA
    return pl.pallas_call(
        backward_kernel,
        out_shape=jax.ShapeDtypeStruct((steps, seqs, block), jnp.bfloat16),
        in_specs=[vmem] * 3 + [hbm] * 2,
        out_specs=vmem,
        scratch_shapes=[
            pltpu.VMEM((full, block), jnp.bfloat16),
            pltpu.VMEM((SLOTS, 4, seqs, block), jnp.bfloat16),
            pltpu.VMEM((seqs, block), jnp.float32),
            pltpu.VMEM((COPIES * seqs, block), jnp.float32),
            dma((4,)), dma((SLOTS, 3, 5)), dma((SLOTS, 3, 5)),
        ],
        compiler_params=pltpu.CompilerParams(collective_id=1, has_side_effects=True, vmem_limit_bytes=60 * 1024 * 1024),
        name="backward",
    )(emit_seq, scales, col, trans_loc, rows_loc)


def solution(mesh):
    def local_run(trans_loc, emit_loc, init_loc, tokens_loc, lengths_loc):
        seqs, steps = tokens_loc.shape
        block = trans_loc.shape[1]
        emit_seq = jnp.transpose(emit_loc.at[:, tokens_loc.T].get(mode="promise_in_bounds"), (1, 2, 0))
        col = lengths_loc[:, None]
        pack = jnp.broadcast_to(lengths_loc.reshape(4, 8).T[:, :, None], (8, 4, 32)).reshape(8, 128)
        alphas, scales, log_sum, last, rows_loc = forward(emit_seq, init_loc, col, pack, trans_loc)
        weights = backward(emit_seq, scales, col, trans_loc, rows_loc)
        pair_sum = lax.dot_general(alphas.reshape(steps * seqs, block), weights.reshape(steps * seqs, block), (((0,), (0,)), ((), ())), preferred_element_type=jnp.float32)
        diag_block = lax.dynamic_slice_in_dim(trans_loc, lax.axis_index('states') * block, block, axis=0)
        counts = diag_block.astype(jnp.float32) * pair_sum
        return log_sum[:, ::32].T.reshape(seqs), last, counts

    return jax.shard_map(local_run, mesh=mesh, in_specs=(P(None, 'states'), P('states', None), P('states'), P('seqs', None), P('seqs')), out_specs=(P('seqs'), P('seqs', 'states'), P(('seqs', 'states'), None)), check_vma=False)
```

profile of v0, /device:TPU:0, one launch (start us, length us, event | category | flops | bytes accessed | tf_op | source)
XLA Modules:
  0.0 1186.0 jit_solution(8824319739938831887)
XLA Ops:
  0.6 0.7 compare_select_fusion
  1.4 0.1 copy.14
  1.4 0.1 reshape.23
  1.5 0.0 copy-start.1
  1.5 47.9 %gather_fusion = bf16[2048,2048]{1,0:T(8,128)(2,1)} fusion(bf16[2048,10000]{0,1:T(8,128)(2,1)} %param.6, s32[2048]{0:T(1024)S(1)} %broadcast_clamp_fusion), kind=kCustom, calls=%fused_computation | custom fusion | bytes 16785408 | tf_op jit(solution)/shard_map/gather | solution.py:365
  49.5 0.0 copy-done.1
  49.5 0.7 copy.16.len_col
  50.2 0.1 reshape.18
  50.2 0.1 copy.15
  50.3 0.1 broadcast_in_dim.18
  50.4 0.7 reshape.19.len_pack
  51.1 648.5 %forward.1 = (bf16[64,32,2048]{2,1,0:T(8,128)(2,1)}, f32[64,8,128]{2,1,0:T(8,128)}, f32[8,128]{1,0:T(8,128)}, f32[32,2048]{1,0:T(8,128)}, bf16[4,2048,2048]{2,1,0:T(8,128)(2,1)}) custom-call(bf16[64,32,2048]{2,1,0:T(8,128)(2,1)} %bitcast.11, f32[1,2048]{1,0:T(1,128)} %bitcast.15, s32[32,1]{1,0:T(8,128)} %copy.16.len_col, s32[8,128]{1,0:T(8,128)} %reshape.19.len_pack, ...), custom_call_target="tpu_custom_call" | custom-call | tf_op jit(solution)/shard_map/forward/pallas_call | solution.py:240
  699.6 0.8 slice.3
  700.3 0.1 copy.17
  700.4 0.6 reshape.20
  701.0 459.1 %backward.1 = bf16[64,32,2048]{2,1,0:T(8,128)(2,1)} custom-call(bf16[64,32,2048]{2,1,0:T(8,128)(2,1)} %bitcast.12, f32[64,8,128]{2,1,0:T(8,128)} %get-tuple-element.11.scale_ref, s32[32,1]{1,0:T(8,128)} %copy.16.len_col, bf16[8192,2048]{1,0:T(8,128)(2,1)} %a_hbm.3, bf16[4,2048,2048]{2,1,0:T(8,128)(2,1)} %get-tuple-element.12.rows_hbm), custom_call_target="tpu_custom_call" | custom-call | tf_op jit(solution)/shard_map/backward/pallas_call | solution.py:344
  1160.1 0.0 copy-start
  1160.1 25.2 %bitcast_multiply_fusion = f32[2048,2048]{1,0:T(8,128)} fusion(bf16[64,32,2048]{2,1,0:T(8,128)(2,1)} %get-tuple-element.10, bf16[64,32,2048]{2,1,0:T(8,128)(2,1)} %backward.1, bf16[8192,2048]{1,0:T(8,128)(2,1)} %a_hbm.3, s32[]{:T(128)S(6)} %select_n.7), kind=kOutput, calls=%fused_computation.1 | convolution fusion | flops 17188257792 | bytes 41943044 | tf_op jit(solution)/shard_map/dot_general | solution.py:370
  1185.3 0.0 copy-done
  1185.3 0.7 copy.24
  (1 shorter events, 0.0 us)
Async XLA Ops:
  1.5 48.0 %copy-start.1 = (s32[32]{0:T(128)S(1)}, s32[32]{0:T(128)}, u32[]{:S(2)}) copy-start(s32[32]{0:T(128)} %param.9) | copy-start | bytes 388
  1160.1 25.2 %copy-start = (f32[32,2048]{1,0:T(8,128)S(1)}, f32[32,2048]{1,0:T(8,128)}, u32[]{:S(2)}) copy-start(f32[32,2048]{1,0:T(8,128)} %get-tuple-element.17) | copy-start | bytes 786436
where the time goes:
time: 1190 us
  Pallas kernels  1110 us (93%)
  local copies, waits for them, and re-layouts  51.9 us (4%)
  matrix products  25.2 us (2%)
    pallas_call x1, Pallas kernels, forward(): pl.pallas_call(forward_kernel, out_shape=[jax.ShapeDtypeStruct((steps, se...  648 us
    pallas_call x1, Pallas kernels, backward(): pl.pallas_call(backward_kernel, out_shape=jax.ShapeDtypeStruct((steps, se...  459 us
    gather x1, local copies, waits for them, and re-layouts, local_run(): emit_loc.at[:, tokens_loc.T].get(mode='promise_in_bounds')  47.9 us
    dot_general x1, matrix products, local_run(): lax.dot_general(alphas.reshape(steps * seqs, block), weights.reshape(step...  25.2 us

commit v1 on v0

--- a/solution.py
+++ b/solution.py
@@ -9,7 +9,11 @@
 LOADS = 8
 TILE = 256
 SLOTS = 4
-COPIES = 4
+FORWARD_COPIES = 1
+BACKWARD_COPIES = 4
+ORDER = (
+    "WP0", "P0", "P1", "P2", "R0", "P3", "C0", "R1", "C1", "WF0", "F0", "R2", "C2", "WF1", "R3", "C3", "R4", "F1", "C4", "WF2", "F2",
+    "WF3", "WF4", "F3", "F4")
 
 
 def entry_barrier(others):
@@ -24,7 +28,8 @@
 
 
 class Exchange:
-    def __init__(self, me, xbuf, mat, acc, send_sem, recv_sem):
+    def __init__(self, me, copies, xbuf, mat, acc, send_sem, recv_sem):
+        self.copies = copies
         self.me, self.xbuf, self.mat, self.acc = me, xbuf, mat, acc
         self.send_sem, self.recv_sem = send_sem, recv_sem
         self.block = xbuf.shape[3]
@@ -53,31 +58,31 @@
             self.copy(slot, self.me, k, 0, self.partner).wait_send()
             self.copy(slot, self.cross, k, 2, self.partner).wait_send()
 
-    def product(self, slot, owner, lo, size, first=False, last=False):
+    def product(self, slot, owner, lo, size, first=False, copies=1):
         lhs = self.xbuf[slot, owner, :, pl.ds(lo, size)]
-        seqs = lhs.shape[0]
         rows = pl.ds(pl.multiple_of(owner * self.block + lo, 128), size)
-        if last:
-            self.acc[:seqs] += jnp.dot(lhs, self.mat[rows, :], preferred_element_type=jnp.float32)
-        else:
-            prod = jnp.dot(jnp.concatenate([lhs] * COPIES, axis=0), self.mat[rows, :], preferred_element_type=jnp.float32)
-            self.acc[...] = prod if first else self.acc[...] + prod
+        prod = jnp.dot(jnp.concatenate([lhs] * copies, axis=0), self.mat[rows, :], preferred_element_type=jnp.float32)
+        out = self.acc.at[:copies * lhs.shape[0]]
+        out[...] = prod if first else out[...] + prod
 
     def run(self, slot, meanwhile):
-        count = len(self.pieces)
         meanwhile()
-        self.product(slot, self.me, 0, self.block, first=True)
-        for k in range(count):
-            self.copy(slot, self.partner, k, 0, self.partner).wait_recv()
-        self.product(slot, self.partner, 0, self.block)
-        for k in range(count + 1):
-            if k < count:
+        self.product(slot, self.me, 0, self.block, True, self.copies)
+        for token in ORDER:
+            what, k = token[:-1], int(token[-1])
+            if what == "WP":
+                for j in range(len(self.pieces)):
+                    self.copy(slot, self.partner, j, 0, self.partner).wait_recv()
+            elif what == "P":
+                self.product(slot, self.partner, k * (self.block // 4), self.block // 4, copies=self.copies)
+            elif what == "R":
                 self.copy(slot, self.cross, k, 1, self.cross).wait_recv()
                 self.copy(slot, self.cross, k, 2, self.partner).start()
-                self.product(slot, self.cross, *self.pieces[k])
-            if k:
-                self.copy(slot, self.far, k - 1, 2, self.partner).wait_recv()
-                self.product(slot, self.far, *self.pieces[k - 1], last=k == count)
+            elif what == "WF":
+                self.copy(slot, self.far, k, 2, self.partner).wait_recv()
+            else:
+                lo, size = self.pieces[k]
+                self.product(slot, self.cross if what == "C" else self.far, lo, size)
 
 
 def packed(col):
@@ -162,7 +167,7 @@
         return cbuf[0] + cbuf[1] + cbuf[2] + cbuf[3]
 
     def body():
-        ex = Exchange(me, xbuf, mat, acc, send_sem, recv_sem)
+        ex = Exchange(me, FORWARD_COPIES, xbuf, mat, acc, send_sem, recv_sem)
         ends = {(lo + size) // TILE - 1: k for k, (lo, size) in enumerate(ex.pieces)}
 
         def finish_step(t, total):
@@ -251,7 +256,7 @@
         scratch_shapes=[
             pltpu.VMEM((full, block), jnp.bfloat16),
             pltpu.VMEM((SLOTS, 4, seqs, block), jnp.bfloat16),
-            pltpu.VMEM((COPIES * seqs, block), jnp.float32),
+            pltpu.VMEM((FORWARD_COPIES * seqs, block), jnp.float32),
             pltpu.VMEM((4, 8, 128), jnp.float32),
             dma((LOADS,)), dma((SLOTS, 3, 5)), dma((SLOTS, 3, 5)), dma((3,)), dma((3,)),
             dma((3, 2)), dma((3, 2)), dma((2, 2)), dma((2,)), dma((2,)), dma,
@@ -301,7 +306,7 @@
             lax.fori_loop(0, side, flip_row, 0)
 
     def body():
-        ex = Exchange(me, xbuf, mat, acc, send_sem, recv_sem)
+        ex = Exchange(me, BACKWARD_COPIES, xbuf, mat, acc, send_sem, recv_sem)
         ends = {(lo + size) // TILE - 1: k for k, (lo, size) in enumerate(ex.pieces)}
 
         def emit_weight(t, n, weight):
@@ -350,7 +355,7 @@
             pltpu.VMEM((full, block), jnp.bfloat16),
             pltpu.VMEM((SLOTS, 4, seqs, block), jnp.bfloat16),
             pltpu.VMEM((seqs, block), jnp.float32),
-            pltpu.VMEM((COPIES * seqs, block), jnp.float32),
+            pltpu.VMEM((BACKWARD_COPIES * seqs, block), jnp.float32),
             dma((4,)), dma((SLOTS, 3, 5)), dma((SLOTS, 3, 5)),
         ],
         compiler_params=pltpu.CompilerParams(collective_id=1, has_side_effects=True, vmem_limit_bytes=60 * 1024 * 1024),
@@ -358,11 +363,61 @@
     )(emit_seq, scales, col, trans_loc, rows_loc)
 
 
+AHEAD = 6
+ROWS = 8
+
+
+def gather_kernel(tok_smem, tok_ref, emit_hbm, out_ref, buf, sem):
+    t = pl.program_id(0)
+    seqs, steps = tok_ref.shape
+
+    def copies(step):
+        slot = step % AHEAD
+        return [pltpu.make_async_copy(
+            emit_hbm.at[pl.ds(pl.multiple_of(tok_smem[b, step] // ROWS * ROWS, ROWS), ROWS)],
+            buf.at[slot, pl.ds(b * ROWS, ROWS)], sem.at[slot, b]) for b in range(seqs)]
+
+    @pl.when(t == 0)
+    def _():
+        for step in range(min(AHEAD - 1, steps)):
+            for c in copies(step):
+                c.start()
+
+    @pl.when(t + AHEAD - 1 < steps)
+    def _():
+        for c in copies(t + AHEAD - 1):
+            c.start()
+
+    for c in copies(t):
+        c.wait()
+    lane = lax.broadcasted_iota(jnp.int32, tok_ref.shape, 1)
+    token = jnp.sum(jnp.where(lane == t, tok_ref[...], 0).astype(jnp.float32), axis=1, keepdims=True).astype(jnp.int32)
+    wide = (seqs, seqs * ROWS)
+    pick = lax.broadcasted_iota(jnp.int32, wide, 0) * ROWS + jnp.broadcast_to(token % ROWS, wide)
+    chosen = jnp.where(lax.broadcasted_iota(jnp.int32, wide, 1) == pick, 1.0, 0.0).astype(jnp.bfloat16)
+    out_ref[0] = jnp.dot(chosen, buf[t % AHEAD], preferred_element_type=jnp.float32).astype(jnp.bfloat16)
+
+
+def gather(emit_loc, tokens_loc):
+    seqs, steps = tokens_loc.shape
+    block = emit_loc.shape[0]
+    return pl.pallas_call(
+        gather_kernel,
+        grid=(steps,),
+        out_shape=jax.ShapeDtypeStruct((steps, seqs, block), jnp.bfloat16),
+        in_specs=[pl.BlockSpec(memory_space=pltpu.SMEM), pl.BlockSpec(memory_space=pltpu.VMEM), pl.BlockSpec(memory_space=pltpu.HBM)],
+        out_specs=pl.BlockSpec((1, seqs, block), lambda t: (t, 0, 0)),
+        scratch_shapes=[pltpu.VMEM((AHEAD, seqs * ROWS, block), jnp.bfloat16), pltpu.SemaphoreType.DMA((AHEAD, seqs))],
+        compiler_params=pltpu.CompilerParams(dimension_semantics=("arbitrary",), vmem_limit_bytes=32 * 1024 * 1024),
+        name="gather",
+    )(tokens_loc, tokens_loc, emit_loc.T)
+
+
 def solution(mesh):
     def local_run(trans_loc, emit_loc, init_loc, tokens_loc, lengths_loc):
         seqs, steps = tokens_loc.shape
         block = trans_loc.shape[1]
-        emit_seq = jnp.transpose(emit_loc.at[:, tokens_loc.T].get(mode="promise_in_bounds"), (1, 2, 0))
+        emit_seq = gather(emit_loc, tokens_loc)
         col = lengths_loc[:, None]
         pack = jnp.broadcast_to(lengths_loc.reshape(4, 8).T[:, :, None], (8, 4, 32)).reshape(8, 128)
         alphas, scales, log_sum, last, rows_loc = forward(emit_seq, init_loc, col, pack, trans_loc)

time: 1190 us -> 1140 us (0.958)
  local copies, waits for them, and re-layouts: 51.9 us -> 7.87 us
    gather x1 -> x0, local copies, waits for them, and re-layouts: 47.9 us -> none  [local_run(): emit_loc.at[:, tokens_loc.T].get(mode='promise_in_bounds')]
    pallas_call x0 -> x1, Pallas kernels: none -> 44.9 us  [gather(): pl.pallas_call(gather_kernel, grid=(steps,), out_shape=jax.ShapeDtypeStru...]
    pallas_call x1, Pallas kernels: 459 us -> 432 us  [backward(): pl.pallas_call(backward_kernel, out_shape=jax.ShapeDtypeStruct((steps, se...]
    pallas_call x1, Pallas kernels: 648 us -> 628 us  [forward(): pl.pallas_call(forward_kernel, out_shape=[jax.ShapeDtypeStruct((steps, se...]
where the time goes in v1:
time: 1140 us
  Pallas kernels  1110 us (97%)
  matrix products  25.2 us (2%)
    pallas_call x1, Pallas kernels, forward(): pl.pallas_call(forward_kernel, out_shape=[jax.ShapeDtypeStruct((steps, se...  628 us
    pallas_call x1, Pallas kernels, backward(): pl.pallas_call(backward_kernel, out_shape=jax.ShapeDtypeStruct((steps, se...  432 us
    pallas_call x1, Pallas kernels, gather(): pl.pallas_call(gather_kernel, grid=(steps,), out_shape=jax.ShapeDtypeStru...  44.9 us
    dot_general x1, matrix products, local_run(): lax.dot_general(alphas.reshape(steps * seqs, block), weights.reshape(step...  25.2 us

profile of v1, /device:TPU:0, one launch (start us, length us, event | category | flops | bytes accessed | tf_op | source)
XLA Modules:
  0.0 1138.9 jit_solution(11139421782271419487)
XLA Ops:
  0.6 0.0 copy-start.1
  0.6 0.7 copy-done.1
  1.3 0.0 copy-start.3
  1.4 44.9 %gather.1.emit_ref = bf16[64,32,2048]{2,1,0:T(8,128)(2,1)S(1)} custom-call(s32[32,64]{1,0:T(8,128)S(1)} %copy-done.1, s32[32,64]{1,0:T(8,128)S(1)} %copy-done.1, bf16[10000,2048]{1,0:T(8,128)(2,1)} %bitcast.9), custom_call_target="tpu_custom_call" | custom-call | tf_op jit(solution)/shard_map/gather/pallas_call | solution.py:404
  46.2 0.0 copy-start
  46.2 3.4 copy-done
  49.6 0.0 copy-done.3
  49.6 0.7 copy.9.len_col
  50.3 0.1 reshape.18
  50.4 0.1 copy.8
  50.5 0.1 broadcast_in_dim.14
  50.6 0.7 reshape.19.len_pack
  51.2 628.3 %forward.1 = (bf16[64,32,2048]{2,1,0:T(8,128)(2,1)}, f32[64,8,128]{2,1,0:T(8,128)}, f32[8,128]{1,0:T(8,128)}, f32[32,2048]{1,0:T(8,128)}, bf16[4,2048,2048]{2,1,0:T(8,128)(2,1)}) custom-call(bf16[64,32,2048]{2,1,0:T(8,128)(2,1)} %copy-done, f32[1,2048]{1,0:T(1,128)} %bitcast.12, s32[32,1]{1,0:T(8,128)} %copy.9.len_col, s32[8,128]{1,0:T(8,128)} %reshape.19.len_pack, ...), custom_call_target="tpu_custom_call" | custom-call | tf_op jit(solution)/shard_map/forward/pallas_call | solution.py:245
  679.5 0.8 slice.3
  680.3 0.1 copy.10
  680.3 0.6 reshape.20
  680.9 431.9 %backward.1 = bf16[64,32,2048]{2,1,0:T(8,128)(2,1)} custom-call(bf16[64,32,2048]{2,1,0:T(8,128)(2,1)} %copy-done, f32[64,8,128]{2,1,0:T(8,128)} %get-tuple-element.11.scale_ref, s32[32,1]{1,0:T(8,128)} %copy.9.len_col, bf16[8192,2048]{1,0:T(8,128)(2,1)} %a_hbm.3, bf16[4,2048,2048]{2,1,0:T(8,128)(2,1)} %get-tuple-element.12.rows_hbm), custom_call_target="tpu_custom_call" | custom-call | tf_op jit(solution)/shard_map/backward/pallas_call | solution.py:349
  1112.9 0.0 copy-start.2
  1112.9 25.2 %bitcast_multiply_fusion = f32[2048,2048]{1,0:T(8,128)} fusion(bf16[64,32,2048]{2,1,0:T(8,128)(2,1)} %get-tuple-element.10, bf16[64,32,2048]{2,1,0:T(8,128)(2,1)} %backward.1, bf16[8192,2048]{1,0:T(8,128)(2,1)} %a_hbm.3, s32[]{:T(128)S(6)} %select_n.3), kind=kOutput, calls=%fused_computation | convolution fusion | flops 17188257792 | bytes 41943044 | tf_op jit(solution)/shard_map/dot_general | solution.py:425
  1138.2 0.0 copy-done.2
  1138.2 0.7 copy.17
Async XLA Ops:
  0.6 0.7 copy-start.1
  1.3 48.3 %copy-start.3 = (s32[32]{0:T(128)S(1)}, s32[32]{0:T(128)}, u32[]{:S(2)}) copy-start(s32[32]{0:T(128)} %param.9) | copy-start | bytes 388
  46.2 3.4 copy-start
  1112.9 25.3 %copy-start.2 = (f32[32,2048]{1,0:T(8,128)S(1)}, f32[32,2048]{1,0:T(8,128)}, u32[]{:S(2)}) copy-start(f32[32,2048]{1,0:T(8,128)} %get-tuple-element.17) | copy-start | bytes 786436
